TPU v7x, 32 devices: a whole 2x2x4 slice. The times are simulated.
32 devices in a mesh: lat: 4 (over y, core), lon: 8 (over z, x).
Axes of the slice: x: 2, y: 2, z: 4, core: 2. Of those that a mesh axis runs over, the one named last changes fastest.
Arguments:
- forcing: float32 [640, 1024], P('lat', 'lon'), may hold values from -28 to 28
- search_direction: float32 [640, 1024], P('lat', 'lon'), may hold values from -28 to 28
- ocean_depth: float32 [640, 1024], P('lat', 'lon'), may hold values from 0.5 to 8
- land_mask: int32 [640, 1024], P('lat', 'lon'), may hold values 0 or 1
- fold_map: int32 [1024], replicated, may hold values from 0 to 1023, as said below
Outputs:
- scaled_height: float32 [640, 1024], P('lat', 'lon')
- residual: float32 [640, 1024], P('lat', 'lon')
Inputs may be any that keep to these rules, and one draw needn't show every extreme that they name: `fold_map`: column j's partner across the fold is (c - j) mod 1024 for one c of 0 to 1023, so the map is its own inverse.
All inputs are finite; a program needn't handle non-finite values. No bound on the sum of `land_mask` on one device may be relied on, other than what follows from the above.
Results may differ from a plain program's by a relative error of at most 0.0003.
Values sent between devices are 32-bit elements; how exact they have to be, the bound alone decides.
A program may use at most 64 MiB of HBM per device.

v0:
```python
import jax
import jax.numpy as jnp
import numpy as np
from jax import lax
from jax.sharding import PartitionSpec as P

STEPS = 8
REACH = 256
PRECISE = lax.Precision.HIGHEST
DIRECTIONS = ((1, 0), (-1, 0), (0, 1), (0, -1), (1, 1), (-1, -1), (1, -1), (-1, 1))
LINK_FACTORS = (1.0, 1.0, 1.0, 1.0, 0.5, 0.5, 0.5, 0.5)


def with_halo(x, sides, width):
    for axis, dim in sides:
        size, length = (lax.axis_size(axis), x.shape[dim])
        up = [(i, (i + 1) % size) for i in range(size)]
        down = [(j, i) for i, j in up]
        last = lax.slice_in_dim(x, length - width, length, axis=dim)
        leading = lax.slice_in_dim(x, 0, width, axis=dim)
        before = lax.ppermute(last, axis, up)
        after = lax.ppermute(leading, axis, down)
        x = jnp.concatenate([before, x, after], axis=dim)
    return x


def chebyshev_table(basis_steps):
    number = 2 * basis_steps + 1
    matrix = np.zeros((number, number), np.float32)
    for offset, length in ((0, basis_steps + 1), (basis_steps + 1, basis_steps)):
        for column in range(length - 1):
            matrix[offset + column, offset + column] = 1.0
            if column == 0:
                matrix[offset + 1, offset] = 1.0
            else:
                matrix[offset + column + 1, offset + column] = 0.5
                matrix[offset + column - 1, offset + column] = 0.5
    return matrix


def coordinates(gram_matrix, basis_steps):
    number = 2 * basis_steps + 1
    shift_matrix = jnp.asarray(chebyshev_table(basis_steps))
    unit_rows = jnp.eye(number, dtype=jnp.float32)
    solution_coords = jnp.zeros((number,), jnp.float32)
    direction_coords = unit_rows[0]
    residual_coords = unit_rows[basis_steps + 1]
    norm_now = jnp.dot(
        residual_coords, jnp.dot(gram_matrix, residual_coords, precision=PRECISE), precision=PRECISE
    )
    for inner_step in range(basis_steps):
        mapped = jnp.dot(shift_matrix, direction_coords, precision=PRECISE)
        curvature = jnp.dot(
            direction_coords, jnp.dot(gram_matrix, mapped, precision=PRECISE), precision=PRECISE
        )
        step_length = norm_now / curvature
        solution_coords = solution_coords + step_length * direction_coords
        residual_coords = residual_coords - step_length * mapped
        norm_next = jnp.dot(
            residual_coords,
            jnp.dot(gram_matrix, residual_coords, precision=PRECISE),
            precision=PRECISE,
        )
        direction_coords = residual_coords + norm_next / norm_now * direction_coords
        norm_now = norm_next
    return (solution_coords, residual_coords, direction_coords)


def trim_margin(source, margin_cells):
    if margin_cells == 0:
        return source
    return source[
        ...,
        margin_cells : source.shape[-2] - margin_cells,
        margin_cells : source.shape[-1] - margin_cells,
    ]


def place_fold(widened, fold_rows, fold_map, margin_cells):
    lat_count = lax.axis_size("lat")
    lat_place = lax.axis_index("lat")
    lon_width = widened.shape[-1] - 2 * margin_cells
    total_columns = fold_map.shape[0]
    columns = (
        lax.axis_index("lon") * lon_width
        - margin_cells
        + jnp.arange(lon_width + 2 * margin_cells, dtype=jnp.int32)
    ) % total_columns
    partners = jnp.take(fold_map, columns)
    mirrored = jnp.take(fold_rows[:, ::-1, :], partners, axis=2)
    north_rows = jnp.where(
        lat_place == lat_count - 1, mirrored, widened[:, widened.shape[1] - margin_cells :, :]
    )
    south_rows = jnp.where(lat_place == 0, 0.0, widened[:, :margin_cells, :])
    return jnp.concatenate(
        [south_rows, widened[:, margin_cells : widened.shape[1] - margin_cells, :], north_rows],
        axis=1,
    )


def extend_depth(fields, fold_map, margin_cells):
    widened = with_halo(fields, (("lat", 1), ("lon", 2)), margin_cells)
    fold_rows = lax.all_gather(
        fields[:, fields.shape[1] - margin_cells :, :], "lon", axis=2, tiled=True
    )
    return place_fold(widened, fold_rows, fold_map, margin_cells)


def extend_full(fields, fold_map, margin_cells):
    widened = with_halo(fields, (("lat", 1), ("lon", 2)), margin_cells)
    fold_rows = lax.all_gather(
        fields[:, fields.shape[1] - margin_cells :, :], "lon", axis=2, tiled=True
    )
    return place_fold(widened, fold_rows, fold_map, margin_cells)


def apply_power(source, source_depth, inverse_root, link_weights):
    outer_cut = STEPS - source_depth
    weighted = source * trim_margin(inverse_root, outer_cut)
    row_total = source.shape[-2] - 2
    column_total = source.shape[-1] - 2
    inner_weights = trim_margin(link_weights, outer_cut + 1)
    running = jnp.zeros((source.shape[0], row_total, column_total), jnp.float32)
    for direction_index in range(8):
        north_step, east_step = DIRECTIONS[direction_index]
        running = (
            running
            + inner_weights[direction_index]
            * weighted[
                :,
                1 + north_step : 1 + north_step + row_total,
                1 + east_step : 1 + east_step + column_total,
            ]
        )
    return -trim_margin(inverse_root, outer_cut + 1) * running


def advance(
    earlier, earlier_depth, current, current_depth, powers, stored, inverse_root, link_weights
):
    for power in powers:
        if power == STEPS - 1:
            earlier = earlier[:1]
            current = current[:1]
        upcoming = 2.0 * apply_power(
            current, current_depth, inverse_root, link_weights
        ) - trim_margin(earlier, earlier_depth - current_depth + 1)
        earlier, earlier_depth = (current, current_depth)
        current, current_depth = (upcoming, current_depth - 1)
        stored.append(trim_margin(current, current_depth))
    return (earlier, earlier_depth, current, current_depth)


def per_device(forcing, search_direction, ocean_depth, land_mask, fold_map):
    ocean_flag = land_mask.astype(jnp.float32)
    column_depth = ocean_depth * ocean_flag
    depth_wide = extend_depth(column_depth[None], fold_map, STEPS + 1)[0]
    wet_wide = (depth_wide > 0.0).astype(jnp.float32)
    centre_depth = trim_margin(depth_wide, 1)
    centre_wet = trim_margin(wet_wide, 1)
    row_total = depth_wide.shape[0] - 2
    column_total = depth_wide.shape[1] - 2
    weight_list = []
    link_sum = jnp.zeros_like(centre_depth)
    for direction_index in range(8):
        north_step, east_step = DIRECTIONS[direction_index]
        beside_depth = depth_wide[
            1 + north_step : 1 + north_step + row_total,
            1 + east_step : 1 + east_step + column_total,
        ]
        beside_wet = wet_wide[
            1 + north_step : 1 + north_step + row_total,
            1 + east_step : 1 + east_step + column_total,
        ]
        weight = (
            LINK_FACTORS[direction_index]
            * 0.5
            * (centre_depth + beside_depth)
            * centre_wet
            * beside_wet
        )
        weight_list.append(weight)
        link_sum = link_sum + weight
    link_weights = jnp.stack(weight_list)
    diagonal = centre_wet * (centre_depth / (REACH * REACH) + link_sum) + (1.0 - centre_wet)
    inverse_root = lax.rsqrt(diagonal)
    scaled_height = jnp.zeros_like(forcing)
    residual = ocean_flag * forcing
    direction = ocean_flag * search_direction
    chains = jnp.stack([direction, residual])
    earlier = extend_full(chains, fold_map, STEPS)
    earlier_depth = STEPS
    current = apply_power(earlier, earlier_depth, inverse_root, link_weights)
    current_depth = earlier_depth - 1
    stored = [trim_margin(earlier, earlier_depth), trim_margin(current, current_depth)]
    advance(
        earlier,
        earlier_depth,
        current,
        current_depth,
        range(1, STEPS),
        stored,
        inverse_root,
        link_weights,
    )
    krylov_basis = jnp.stack(
        [member[0] for member in stored] + [member[1] for member in stored[:STEPS]]
    )
    flattened = krylov_basis.reshape(krylov_basis.shape[0], -1)
    partial_gram = jnp.dot(flattened, flattened.T, precision=PRECISE)
    gram_matrix = lax.psum(partial_gram, ("lat", "lon"))
    solution_coords, residual_coords, direction_coords = coordinates(gram_matrix, STEPS)
    scaled_height = scaled_height + jnp.einsum(
        "k,kij->ij", solution_coords, krylov_basis, precision=PRECISE
    )
    residual = jnp.einsum("k,kij->ij", residual_coords, krylov_basis, precision=PRECISE)
    return (scaled_height, residual)


def solution(mesh):
    in_specs = (P("lat", "lon"), P("lat", "lon"), P("lat", "lon"), P("lat", "lon"), P())
    out_specs = (P("lat", "lon"), P("lat", "lon"))
    return jax.shard_map(
        per_device, mesh=mesh, in_specs=in_specs, out_specs=out_specs, check_vma=False
    )
```

profile of v0, /device:TPU:14, one launch (start us, length us, event | category | flops | bytes accessed | tf_op | source)
XLA Modules:
  0.0 225.7 jit_solution(7884336896558490846)
XLA Ops:
  0.7 1.0 copy.157
  5.4 1.7 collective-permute-start.1
  7.6 1.0 fusion.110
  8.6 1.7 collective-permute-start.5
  11.1 1.2 gather_fusion
  13.4 28.1 %all_gather.7 = f32[2,8,1024]{2,1,0:T(8,128)S(1)} all-gather(f32[2,8,128]{2,1,0:T(8,128)S(1)} %copy.165), channel_id=1, replica_groups=mesh['lat'=4,'lon'=8] {'lon'}, dimensions={2}, use_global_device_ids=true | all-gather | bytes 73728 | tf_op jit(solution)/shard_map/all_gather | solution.py:111
  41.5 1.2 gather_fusion.2
  44.5 31.5 %all_gather.6 = f32[1,9,1024]{1,2,0:T(8,128)S(1)} all-gather(f32[1,9,128]{1,2,0:T(8,128)} %get-tuple-element.75), channel_id=1, replica_groups=mesh['lat'=4,'lon'=8] {'lon'}, dimensions={2}, use_global_device_ids=true | all-gather | bytes 41472 | tf_op jit(solution)/shard_map/all_gather | solution.py:103
  77.3 2.3 %rev.7 = f32[2,8,1024]{1,0,2:T(2,128)S(1)} reverse(f32[2,8,1024]{1,0,2:T(2,128)S(1)} %copy.166), dimensions={1} | reverse | bytes 131072 | tf_op jit(solution)/shard_map/rev | solution.py:90
  81.5 2.0 collective-permute-start.3
  83.7 1.9 collective-permute-start.6
  85.6 1.2 collective-permute-start.7
  98.4 2.9 %broadcast_multiply_fusion.1 = (f32[2,174,142]{1,0,2:T(2,128)S(1)}, f32[2,174,142]{1,0,2:T(2,128)S(1)}) fusion(f32[174,142]{0,1:T(8,128)S(1)} %get-tuple-element.65, f32[2,176,144]{1,0,2:T(2,128)S(1)} %get-tuple-element.14, f32[174,142]{0,1:T(8,128)S(1)} %get-tuple-element.77, f32[174,142]{0,1:T(8,128)S(1)} %get-tuple-element.84, ...), kind=kLoop, calls=%fused_computation.244 | loop fusion | flops 840072 | bytes 2964960 | tf_op jit(solution)/shard_map/mul | solution.py:119
  101.3 1.2 fusion.197
  102.5 2.6 %broadcast_multiply_fusion.2 = (f32[2,172,140]{1,0,2:T(2,128)S(1)}, f32[2,172,140]{1,0,2:T(2,128)S(1)}) fusion(f32[172,140]{0,1:T(8,128)S(1)} %get-tuple-element.63, f32[2,176,144]{1,0,2:T(2,128)S(1)} %get-tuple-element.15, f32[2,174,142]{1,0,2:T(2,128)S(1)} %get-tuple-element.12, f32[172,140]{0,1:T(8,128)S(1)} %get-tuple-element.85, ...), kind=kLoop, calls=%fused_computation.245 | loop fusion | flops 915040 | bytes 3082240 | tf_op jit(solution)/shard_map/mul | solution.py:119
  105.2 2.6 %broadcast_multiply_fusion.3 = (f32[2,170,138]{1,0,2:T(2,128)S(1)}, f32[2,170,138]{1,0,2:T(2,128)S(1)}) fusion(f32[170,138]{0,1:T(8,128)S(1)} %get-tuple-element.61, f32[2,174,142]{1,0,2:T(2,128)S(1)} %get-tuple-element.13, f32[2,172,140]{1,0,2:T(2,128)S(1)} %get-tuple-element.10, f32[170,138]{0,1:T(8,128)S(1)} %get-tuple-element.93, ...), kind=kLoop, calls=%fused_computation.246 | loop fusion | flops 891480 | bytes 3002880 | tf_op jit(solution)/shard_map/mul | solution.py:119
  107.8 1.3 fusion.199
  109.1 1.3 fusion.198
  110.4 2.5 %broadcast_multiply_fusion.4 = (f32[2,168,136]{1,0,2:T(2,128)S(1)}, f32[2,168,136]{1,0,2:T(2,128)S(1)}) fusion(f32[168,136]{0,1:T(8,128)S(1)} %get-tuple-element.59, f32[2,172,140]{1,0,2:T(2,128)S(1)} %get-tuple-element.11, f32[2,170,138]{1,0,2:T(2,128)S(1)} %get-tuple-element.8, f32[168,136]{0,1:T(8,128)S(1)} %get-tuple-element.101, ...), kind=kLoop, calls=%fused_computation.279 | loop fusion | flops 868224 | bytes 2924544 | tf_op jit(solution)/shard_map/mul | solution.py:119
  113.0 2.6 %broadcast_multiply_fusion.5 = (f32[2,166,134]{1,0,2:T(2,128)S(1)}, f32[2,166,134]{1,0,2:T(2,128)S(1)}) fusion(f32[166,134]{0,1:T(8,128)S(1)} %get-tuple-element.57, f32[2,170,138]{1,0,2:T(2,128)S(1)} %get-tuple-element.9, f32[2,168,136]{1,0,2:T(2,128)S(1)} %get-tuple-element.6, f32[166,134]{0,1:T(8,128)S(1)} %get-tuple-element.109, ...), kind=kLoop, calls=%fused_computation.280 | loop fusion | flops 845272 | bytes 2847232 | tf_op jit(solution)/shard_map/mul | solution.py:119
  115.6 1.3 fusion.201
  116.9 1.3 fusion.200
  118.2 2.5 %broadcast_multiply_fusion.6 = (f32[2,164,132]{1,0,2:T(2,128)S(1)}, f32[2,164,132]{1,0,2:T(2,128)S(1)}) fusion(f32[164,132]{0,1:T(8,128)S(1)} %get-tuple-element.55, f32[2,168,136]{1,0,2:T(2,128)S(1)} %get-tuple-element.7, f32[2,166,134]{1,0,2:T(2,128)S(1)} %get-tuple-element.4, f32[164,132]{0,1:T(8,128)S(1)} %get-tuple-element.117, ...), kind=kLoop, calls=%fused_computation.281 | loop fusion | flops 822624 | bytes 2770944 | tf_op jit(solution)/shard_map/mul | solution.py:119
  120.7 2.6 %slice_subtract_fusion.5 = f32[2,162,130]{1,0,2:T(2,128)S(1)} fusion(f32[2,166,134]{1,0,2:T(2,128)S(1)} %get-tuple-element.5, f32[2,164,132]{1,0,2:T(2,128)S(1)} %get-tuple-element.2, f32[162,130]{0,1:T(8,128)S(1)} %get-tuple-element.125, f32[162,130]{0,1:T(8,128)S(1)} %get-tuple-element.132, f32[162,130]{0,1:T(8,128)S(1)} %get-tuple-element.126, ...), kind=kLoop, calls=%fused_computation.161 | loop fusion | flops 758160 | bytes 2442960 | tf_op jit(solution)/shard_map/sub | solution.py:145
  123.3 1.3 fusion.203
  124.8 1.2 fusion.204
  126.3 1.9 fusion.202
  128.2 7.4 %stack.48 = f32[17,160,128]{1,0,2:T(8,128)S(1)} concatenate(f32[1,160,128]{1,0,2:T(1,128)S(1)} %copy.178, f32[1,160,128]{1,0,2:T(1,128)} %get-tuple-element.32, f32[1,160,128]{1,0,2:T(1,128)} %get-tuple-element.34, f32[1,160,128]{1,0,2:T(1,128)} %get-tuple-element.36, f32[1,160,128]{1,0,2:T(1,128)} %get-tuple-element.38, f32[1,160,128]{1,0,2:T(1,128)} %get-tuple-element.40, ...), dimensions={0} | concatenate | bytes 2785280 | tf_op jit(solution)/shard_map/stack | solution.py:206
  135.6 3.4 %convolution_bitcast_fusion = f32[17,17]{1,0:T(8,128)S(1)} fusion(f32[17,160,128]{1,0,2:T(8,128)S(1)} %stack.48), kind=kOutput, calls=%fused_computation.4 | convolution fusion | flops 71024640 | bytes 1393796 | tf_op jit(solution)/shard_map/dot_general | solution.py:210
  139.0 46.3 %psum.7 = f32[17,17]{1,0:T(8,128)S(1)} all-reduce(f32[17,17]{1,0:T(8,128)S(1)} %convolution_bitcast_fusion), channel_id=1, replica_groups=mesh['lat'=4,'lon'=8] {'lat','lon'}, use_global_device_ids=true, to_apply=%region_0.1 | all-reduce | flops 289 | bytes 2312 | tf_op jit(solution)/shard_map/psum | solution.py:211
  219.8 1.7 fusion.131
  221.5 2.4 %fusion.133 = f32[1,160,128]{1,0,2:T(1,128)S(1)} fusion(f32[17,160,128]{1,0,2:T(8,128)S(1)} %stack.48, f32[17]{0:T(128)S(1)} %multiply_add_fusion, f32[17]{0:T(128)S(1)} %multiply_add_fusion.1, f32[17]{0:T(128)S(1)} %multiply_add_fusion.2, f32[17]{0:T(128)S(1)} %multiply_add_fusion.3, f32[17]{0:T(128)S(1)} %multiply_add_fusion.4, ...), kind=kOutput, calls=%fused_computation.364 | convolution fusion | flops 4178175 | bytes 1475580 | tf_op jit(solution)/shard_map/k,kij->ij/dot_general | solution.py:213
  (151 shorter events, 38.5 us)
Async XLA Ops:
  0.6 10.4 %copy-start = (s32[1024]{0:T(1024)S(1)}, s32[1024]{0:T(1024)}, u32[]{:S(2)}) copy-start(s32[1024]{0:T(1024)} %param.10) | copy-start | bytes 12292
  0.6 43.2 %copy-start.1 = (f32[17,17]{1,0:T(8,128)S(1)}, f32[17,17]{1,0:T(8,128)}, u32[]{:S(2)}) copy-start(f32[17,17]{1,0:T(8,128)} %constant.118.clone) | copy-start | bytes 3472
  5.4 76.0 %collective-permute-start = (f32[1,9,128]{1,2,0:T(8,128)}, f32[1,9,128]{1,2,0:T(8,128)S(1)}, u32[]{:S(2)}, u32[]{:S(2)}) collective-permute-start(f32[1,9,128]{1,2,0:T(8,128)} %get-tuple-element.75), channel_id=1, source_target_pairs={{0,8},{8,16},{16,24},{24,0},{1,9},{9,17},{17,25},{25,1},{2,10},{10... | collective-permute-start | bytes 13832 | tf_op jit(solution)/shard_map/ppermute | solution.py:21
  5.4 76.0 %collective-permute-start.1 = (f32[1,9,128]{1,2,0:T(8,128)}, f32[1,9,128]{1,2,0:T(8,128)S(1)}, u32[]{:S(2)}, u32[]{:S(2)}) collective-permute-start(f32[1,9,128]{1,2,0:T(8,128)} %get-tuple-element.76), channel_id=1, source_target_pairs={{8,0},{16,8},{24,16},{0,24},{9,1},{17,9},{25,17},{1,25},{10,2},{18... | collective-permute-start | bytes 13832 | tf_op jit(solution)/shard_map/ppermute | solution.py:22
  8.6 74.9 %collective-permute-start.4 = (f32[2,8,128]{1,0,2:T(2,128)S(1)}, f32[2,8,128]{1,0,2:T(2,128)S(1)}, u32[]{:S(2)}, u32[]{:S(2)}) collective-permute-start(f32[2,8,128]{1,0,2:T(2,128)S(1)} %get-tuple-element.46), channel_id=1, source_target_pairs={{0,8},{8,16},{16,24},{24,0},{1,9},{9,17},{17,25},{25,1},{2,10},{10... | collective-permute-start | bytes 24584 | tf_op jit(solution)/shard_map/ppermute | solution.py:21
  8.6 74.9 %collective-permute-start.5 = (f32[2,8,128]{1,0,2:T(2,128)}, f32[2,8,128]{1,0,2:T(2,128)S(1)}, u32[]{:S(2)}, u32[]{:S(2)}) collective-permute-start(f32[2,8,128]{1,0,2:T(2,128)} %get-tuple-element.47), channel_id=1, source_target_pairs={{8,0},{16,8},{24,16},{0,24},{9,1},{17,9},{25,17},{1,25},{10,2},{18... | collective-permute-start | bytes 24584 | tf_op jit(solution)/shard_map/ppermute | solution.py:22
  10.4 34.1 %copy-start.4 = (pred[17,17]{1,0:T(8,128)(4,1)}, pred[17,17]{1,0:T(8,128)(4,1)S(1)}, u32[]{:S(2)}) copy-start(pred[17,17]{1,0:T(8,128)(4,1)S(1)} %iota_compare_fusion) | copy-start | bytes 871
  81.4 5.4 %collective-permute-start.2 = (f32[1,178,9]{1,2,0:T(8,128)S(1)}, f32[1,178,9]{1,2,0:T(8,128)S(1)}, u32[]{:S(2)}, u32[]{:S(2)}) collective-permute-start(f32[1,178,9]{1,2,0:T(8,128)S(1)} %get-tuple-element.48), channel_id=1, source_target_pairs={{0,1},{1,2},{2,3},{3,4},{4,5},{5,6},{6,7},{7,0},{8,9},{9,10},{10,1... | collective-permute-start | bytes 19232 | tf_op jit(solution)/shard_map/ppermute | solution.py:21
  81.5 5.6 %collective-permute-start.3 = (f32[1,178,9]{1,2,0:T(8,128)S(1)}, f32[1,178,9]{1,2,0:T(8,128)S(1)}, u32[]{:S(2)}, u32[]{:S(2)}) collective-permute-start(f32[1,178,9]{1,2,0:T(8,128)S(1)} %get-tuple-element.49), channel_id=1, source_target_pairs={{1,0},{2,1},{3,2},{4,3},{5,4},{6,5},{7,6},{0,7},{9,8},{10,9},{11,1... | collective-permute-start | bytes 19232 | tf_op jit(solution)/shard_map/ppermute | solution.py:22
  83.5 5.2 %copy-start.2 = (f32[2,8,128]{1,0,2:T(2,128)}, f32[2,8,128]{1,0,2:T(2,128)S(1)}, u32[]{:S(2)}) copy-start(f32[2,8,128]{1,0,2:T(2,128)S(1)} %collective-permute-done.5) | copy-start | bytes 24580
  83.7 12.6 %collective-permute-start.6 = (f32[2,176,8]{1,0,2:T(2,128)S(1)}, f32[2,176,8]{1,0,2:T(2,128)S(1)}, u32[]{:S(2)}, u32[]{:S(2)}) collective-permute-start(f32[2,176,8]{1,0,2:T(2,128)S(1)} %get-tuple-element.27), channel_id=1, source_target_pairs={{0,1},{1,2},{2,3},{3,4},{4,5},{5,6},{6,7},{7,0},{8,9},{9,10},{10,1... | collective-permute-start | bytes 33800 | tf_op jit(solution)/shard_map/ppermute | solution.py:21
  85.6 10.6 %collective-permute-start.7 = (f32[2,176,8]{1,0,2:T(2,128)S(1)}, f32[2,176,8]{1,0,2:T(2,128)S(1)}, u32[]{:S(2)}, u32[]{:S(2)}) collective-permute-start(f32[2,176,8]{1,0,2:T(2,128)S(1)} %get-tuple-element.28), channel_id=1, source_target_pairs={{1,0},{2,1},{3,2},{4,3},{5,4},{6,5},{7,6},{0,7},{9,8},{10,9},{11,1... | collective-permute-start | bytes 33800 | tf_op jit(solution)/shard_map/ppermute | solution.py:22
  94.9 1.4 copy-start.3
  95.2 2.2 copy-start.7
  135.6 49.7 %copy-start.5 = (pred[17,17]{1,0:T(8,128)(4,1)S(1)}, pred[17,17]{1,0:T(8,128)(4,1)}, u32[]{:S(2)}) copy-start(pred[17,17]{1,0:T(8,128)(4,1)} %copy-done.4) | copy-start | bytes 871
  135.6 50.4 %copy-start.6 = (f32[1,17]{1,0:T(1,128)S(1)}, f32[1,17]{1,0:T(1,128)}, u32[]{:S(2)}) copy-start(f32[1,17]{1,0:T(1,128)} %fusion.123) | copy-start | bytes 208
where the time goes:
time: 230 us; the launch traced here: 226 us
  blocking collectives  106 us (46%)
  local copies, waits for them, and re-layouts  37.6 us (16%)
  other arithmetic  30.4 us (13%)
  between operations  21.8 us (9%)
  matrix products  21.1 us (9%)
  starting transfers between devices  8.72 us (4%)
    psum x1, blocking collectives, per_device(): gram_matrix = lax.psum(partial_gram, ('lat', 'lon'))  46.3 us
    all_gather x1, blocking collectives, extend_depth(): lax.all_gather(fields[:, fields.shape[1] - margin_cells:, :], 'lon', axis...  31.5 us
    all_gather x1, blocking collectives, extend_full(): lax.all_gather(fields[:, fields.shape[1] - margin_cells:, :], 'lon', axis...  28.1 us
    mul x8, other arithmetic, apply_power(): weighted = source * trim_margin(inverse_root, outer_cut)  16.5 us
    slice x6, local copies, waits for them, and re-layouts, per_device(): member[1]  7.88 us
    another operation x1, local copies, waits for them, and re-layouts, per_device(): jnp.stack([member[0] for member in stored] + [member[1] for member in sto...  7.44 us
    ppermute x4, starting transfers between devices, with_halo(): after = lax.ppermute(leading, axis, down)  6.73 us
    dot_general x8, matrix products, coordinates(): jnp.dot(gram_matrix, mapped, precision=PRECISE)  6.05 us
  transfers between devices with their start and end apart: 8, of which 1 were waited for; matrix products, arithmetic and copies ran while one was open for 10% of the time, Pallas kernels for 0%

commit v1 on v0

--- a/solution.py
+++ b/solution.py
@@ -208,7 +208,7 @@
     )
     flattened = krylov_basis.reshape(krylov_basis.shape[0], -1)
     partial_gram = jnp.dot(flattened, flattened.T, precision=PRECISE)
-    gram_matrix = lax.psum(partial_gram, ("lat", "lon"))
+    gram_matrix = jnp.sum(lax.all_gather(partial_gram, ("lat", "lon")), axis=0)
     solution_coords, residual_coords, direction_coords = coordinates(gram_matrix, STEPS)
     scaled_height = scaled_height + jnp.einsum(
         "k,kij->ij", solution_coords, krylov_basis, precision=PRECISE

time: 230 us -> 266 us (1.16)
  the two profiles are of different devices: /device:TPU:14 before, /device:TPU:0 now
where the time goes in v1:
time: 266 us; the launch traced here: 261 us
  blocking collectives  129 us (48%)
  local copies, waits for them, and re-layouts  38 us (14%)
  other arithmetic  30.3 us (11%)
  matrix products  27.6 us (10%)
  between operations  21.8 us (8%)
  starting transfers between devices  14 us (5%)
    all_gather x1, blocking collectives, per_device(): gram_matrix = jnp.sum(lax.all_gather(partial_gram, ('lat', 'lon')), axis=0)  65.9 us
    all_gather x1, blocking collectives, extend_full(): lax.all_gather(fields[:, fields.shape[1] - margin_cells:, :], 'lon', axis...  31.7 us
    all_gather x1, blocking collectives, extend_depth(): lax.all_gather(fields[:, fields.shape[1] - margin_cells:, :], 'lon', axis...  31.4 us
    mul x8, other arithmetic, apply_power(): weighted = source * trim_margin(inverse_root, outer_cut)  16.5 us
    ppermute x4, starting transfers between devices, with_halo(): after = lax.ppermute(leading, axis, down)  11 us
    slice x6, local copies, waits for them, and re-layouts, per_device(): member[1]  7.92 us
    another operation x1, local copies, waits for them, and re-layouts, per_device(): jnp.stack([member[0] for member in stored] + [member[1] for member in sto...  7.44 us
    dot_general x8, matrix products, coordinates(): jnp.dot(gram_matrix, mapped, precision=PRECISE)  6.74 us
  transfers between devices with their start and end apart: 8, of which 0 were waited for; matrix products, arithmetic and copies ran while one was open for 8% of the time, Pallas kernels for 0%

profile of v1, /device:TPU:0, one launch (start us, length us, event | category | flops | bytes accessed | tf_op | source)
XLA Modules:
  0.0 260.7 jit_solution(1003614047794175117)
XLA Ops:
  5.9 1.9 collective-permute-start.1
  11.8 1.2 gather_fusion
  13.6 31.7 %all_gather.13 = f32[2,8,1024]{2,1,0:T(8,128)S(1)} all-gather(f32[2,8,128]{2,1,0:T(8,128)S(1)} %copy.182), channel_id=1, replica_groups=mesh['lat'=4,'lon'=8] {'lon'}, dimensions={2}, use_global_device_ids=true | all-gather | bytes 73728 | tf_op jit(solution)/shard_map/all_gather | solution.py:111
  45.2 1.2 gather_fusion.2
  47.2 31.4 %all_gather.12 = f32[1,9,1024]{1,2,0:T(8,128)S(1)} all-gather(f32[1,9,128]{1,2,0:T(8,128)} %get-tuple-element.75), channel_id=1, replica_groups=mesh['lat'=4,'lon'=8] {'lon'}, dimensions={2}, use_global_device_ids=true | all-gather | bytes 41472 | tf_op jit(solution)/shard_map/all_gather | solution.py:103
  79.8 2.4 rev.7
  82.9 1.5 gather_fusion.3
  85.1 1.8 collective-permute-start.2
  87.0 3.0 %collective-permute-start.3 = (f32[1,178,9]{1,2,0:T(8,128)S(1)}, f32[1,178,9]{1,2,0:T(8,128)S(1)}, u32[]{:S(2)}, u32[]{:S(2)}) collective-permute-start(f32[1,178,9]{1,2,0:T(8,128)S(1)} %get-tuple-element.49), channel_id=1, source_target_pairs={{1,0},{2,1},{3,2},{4,3},{5,4},{6,5},{7,6},{0,7},{9,8},{10,9},{11,1... | collective-permute-start | bytes 19232 | tf_op jit(solution)/shard_map/ppermute | solution.py:22
  90.2 5.0 %collective-permute-start.7 = (f32[2,176,8]{1,0,2:T(2,128)S(1)}, f32[2,176,8]{1,0,2:T(2,128)S(1)}, u32[]{:S(2)}, u32[]{:S(2)}) collective-permute-start(f32[2,176,8]{1,0,2:T(2,128)S(1)} %get-tuple-element.28), channel_id=1, source_target_pairs={{1,0},{2,1},{3,2},{4,3},{5,4},{6,5},{7,6},{0,7},{9,8},{10,9},{11,1... | collective-permute-start | bytes 33800 | tf_op jit(solution)/shard_map/ppermute | solution.py:22
  107.3 2.9 %broadcast_multiply_fusion.1 = (f32[2,174,142]{1,0,2:T(2,128)S(1)}, f32[2,174,142]{1,0,2:T(2,128)S(1)}) fusion(f32[174,142]{0,1:T(8,128)S(1)} %get-tuple-element.65, f32[2,176,144]{1,0,2:T(2,128)S(1)} %get-tuple-element.14, f32[174,142]{0,1:T(8,128)S(1)} %get-tuple-element.77, f32[174,142]{0,1:T(8,128)S(1)} %get-tuple-element.84, ...), kind=kLoop, calls=%fused_computation.244 | loop fusion | flops 840072 | bytes 2964960 | tf_op jit(solution)/shard_map/mul | solution.py:119
  110.2 1.2 fusion.197
  111.4 2.6 %broadcast_multiply_fusion.2 = (f32[2,172,140]{1,0,2:T(2,128)S(1)}, f32[2,172,140]{1,0,2:T(2,128)S(1)}) fusion(f32[172,140]{0,1:T(8,128)S(1)} %get-tuple-element.63, f32[2,176,144]{1,0,2:T(2,128)S(1)} %get-tuple-element.15, f32[2,174,142]{1,0,2:T(2,128)S(1)} %get-tuple-element.12, f32[172,140]{0,1:T(8,128)S(1)} %get-tuple-element.85, ...), kind=kLoop, calls=%fused_computation.245 | loop fusion | flops 915040 | bytes 3082240 | tf_op jit(solution)/shard_map/mul | solution.py:119
  114.0 2.6 %broadcast_multiply_fusion.3 = (f32[2,170,138]{1,0,2:T(2,128)S(1)}, f32[2,170,138]{1,0,2:T(2,128)S(1)}) fusion(f32[170,138]{0,1:T(8,128)S(1)} %get-tuple-element.61, f32[2,174,142]{1,0,2:T(2,128)S(1)} %get-tuple-element.13, f32[2,172,140]{1,0,2:T(2,128)S(1)} %get-tuple-element.10, f32[170,138]{0,1:T(8,128)S(1)} %get-tuple-element.93, ...), kind=kLoop, calls=%fused_computation.246 | loop fusion | flops 891480 | bytes 3002880 | tf_op jit(solution)/shard_map/mul | solution.py:119
  116.7 1.3 fusion.199
  118.0 1.3 fusion.198
  119.3 2.6 broadcast_multiply_fusion.4
  121.9 2.6 broadcast_multiply_fusion.5
  124.5 1.3 fusion.201
  125.8 1.3 fusion.200
  127.1 2.5 broadcast_multiply_fusion.6
  129.6 2.6 slice_subtract_fusion.5
  132.2 1.3 fusion.203
  133.7 1.2 fusion.204
  135.2 1.9 fusion.202
  137.1 7.4 %stack.48 = f32[17,160,128]{1,0,2:T(8,128)S(1)} concatenate(f32[1,160,128]{1,0,2:T(1,128)S(1)} %copy.195, f32[1,160,128]{1,0,2:T(1,128)} %get-tuple-element.32, f32[1,160,128]{1,0,2:T(1,128)} %get-tuple-element.34, f32[1,160,128]{1,0,2:T(1,128)} %get-tuple-element.36, f32[1,160,128]{1,0,2:T(1,128)} %get-tuple-element.38, f32[1,160,128]{1,0,2:T(1,128)} %get-tuple-element.40, ...), dimensions={0} | concatenate | bytes 2785280 | tf_op jit(solution)/shard_map/stack | solution.py:206
  144.6 3.4 %convolution_bitcast_fusion = f32[1,17,17]{2,1,0:T(8,128)S(1)} fusion(f32[17,160,128]{1,0,2:T(8,128)S(1)} %stack.48), kind=kOutput, calls=%fused_computation.4 | convolution fusion | flops 71024640 | bytes 1393796 | tf_op jit(solution)/shard_map/dot_general | solution.py:210
  147.9 65.9 %all-gather.1 = f32[32,17,17]{2,1,0:T(8,128)S(1)} all-gather(f32[1,17,17]{2,1,0:T(8,128)S(1)} %convolution_bitcast_fusion), channel_id=2, replica_groups=mesh['lat'=4,'lon'=8] {'lat','lon'}, dimensions={0}, use_global_device_ids=true | all-gather | bytes 38148 | tf_op jit(solution)/shard_map/all_gather | solution.py:211
  213.9 1.5 fusion.17
  215.3 1.4 fusion.16
  254.7 1.8 fusion.131
  256.5 2.4 fusion.133
  (148 shorter events, 44.9 us)
Async XLA Ops:
  0.6 11.1 %copy-start = (s32[1024]{0:T(1024)S(1)}, s32[1024]{0:T(1024)}, u32[]{:S(2)}) copy-start(s32[1024]{0:T(1024)} %param.10) | copy-start | bytes 12292
  0.6 45.8 %copy-start.1 = (f32[17,17]{1,0:T(8,128)S(1)}, f32[17,17]{1,0:T(8,128)}, u32[]{:S(2)}) copy-start(f32[17,17]{1,0:T(8,128)} %constant.118.clone) | copy-start | bytes 3472
  5.4 78.9 %collective-permute-start = (f32[1,9,128]{1,2,0:T(8,128)}, f32[1,9,128]{1,2,0:T(8,128)S(1)}, u32[]{:S(2)}, u32[]{:S(2)}) collective-permute-start(f32[1,9,128]{1,2,0:T(8,128)} %get-tuple-element.75), channel_id=1, source_target_pairs={{0,8},{8,16},{16,24},{24,0},{1,9},{9,17},{17,25},{25,1},{2,10},{10... | collective-permute-start | bytes 13832 | tf_op jit(solution)/shard_map/ppermute | solution.py:21
  5.9 78.5 %collective-permute-start.1 = (f32[1,9,128]{1,2,0:T(8,128)}, f32[1,9,128]{1,2,0:T(8,128)}, u32[]{:S(2)}, u32[]{:S(2)}) collective-permute-start(f32[1,9,128]{1,2,0:T(8,128)} %get-tuple-element.76), channel_id=1, source_target_pairs={{8,0},{16,8},{24,16},{0,24},{9,1},{17,9},{25,17},{1,25},{10,2},{18... | collective-permute-start | bytes 13832 | tf_op jit(solution)/shard_map/ppermute | solution.py:22
  9.3 80.6 %collective-permute-start.4 = (f32[2,8,128]{1,0,2:T(2,128)S(1)}, f32[2,8,128]{1,0,2:T(2,128)S(1)}, u32[]{:S(2)}, u32[]{:S(2)}) collective-permute-start(f32[2,8,128]{1,0,2:T(2,128)S(1)} %get-tuple-element.46), channel_id=1, source_target_pairs={{0,8},{8,16},{16,24},{24,0},{1,9},{9,17},{17,25},{25,1},{2,10},{10... | collective-permute-start | bytes 24584 | tf_op jit(solution)/shard_map/ppermute | solution.py:21
  10.0 79.9 %collective-permute-start.5 = (f32[2,8,128]{1,0,2:T(2,128)}, f32[2,8,128]{1,0,2:T(2,128)S(1)}, u32[]{:S(2)}, u32[]{:S(2)}) collective-permute-start(f32[2,8,128]{1,0,2:T(2,128)} %get-tuple-element.47), channel_id=1, source_target_pairs={{8,0},{16,8},{24,16},{0,24},{9,1},{17,9},{25,17},{1,25},{10,2},{18... | collective-permute-start | bytes 24584 | tf_op jit(solution)/shard_map/ppermute | solution.py:22
  11.1 35.4 %copy-start.5 = (pred[17,17]{1,0:T(8,128)(4,1)}, pred[17,17]{1,0:T(8,128)(4,1)S(1)}, u32[]{:S(2)}) copy-start(pred[17,17]{1,0:T(8,128)(4,1)S(1)} %iota_compare_fusion) | copy-start | bytes 871
  85.1 10.0 %collective-permute-start.2 = (f32[1,178,9]{1,2,0:T(8,128)S(1)}, f32[1,178,9]{1,2,0:T(8,128)S(1)}, u32[]{:S(2)}, u32[]{:S(2)}) collective-permute-start(f32[1,178,9]{1,2,0:T(8,128)S(1)} %get-tuple-element.48), channel_id=1, source_target_pairs={{0,1},{1,2},{2,3},{3,4},{4,5},{5,6},{6,7},{7,0},{8,9},{9,10},{10,1... | collective-permute-start | bytes 19232 | tf_op jit(solution)/shard_map/ppermute | solution.py:21
  87.0 8.2 %collective-permute-start.3 = (f32[1,178,9]{1,2,0:T(8,128)S(1)}, f32[1,178,9]{1,2,0:T(8,128)S(1)}, u32[]{:S(2)}, u32[]{:S(2)}) collective-permute-start(f32[1,178,9]{1,2,0:T(8,128)S(1)} %get-tuple-element.49), channel_id=1, source_target_pairs={{1,0},{2,1},{3,2},{4,3},{5,4},{6,5},{7,6},{0,7},{9,8},{10,9},{11,1... | collective-permute-start | bytes 19232 | tf_op jit(solution)/shard_map/ppermute | solution.py:22
  89.9 7.7 %copy-start.2 = (f32[2,8,128]{1,0,2:T(2,128)}, f32[2,8,128]{1,0,2:T(2,128)S(1)}, u32[]{:S(2)}) copy-start(f32[2,8,128]{1,0,2:T(2,128)S(1)} %collective-permute-done.5) | copy-start | bytes 24580
  90.1 15.0 %collective-permute-start.6 = (f32[2,176,8]{1,0,2:T(2,128)S(1)}, f32[2,176,8]{1,0,2:T(2,128)S(1)}, u32[]{:S(2)}, u32[]{:S(2)}) collective-permute-start(f32[2,176,8]{1,0,2:T(2,128)S(1)} %get-tuple-element.27), channel_id=1, source_target_pairs={{0,1},{1,2},{2,3},{3,4},{4,5},{5,6},{6,7},{7,0},{8,9},{9,10},{10,1... | collective-permute-start | bytes 33800 | tf_op jit(solution)/shard_map/ppermute | solution.py:21
  90.2 15.0 %collective-permute-start.7 = (f32[2,176,8]{1,0,2:T(2,128)S(1)}, f32[2,176,8]{1,0,2:T(2,128)S(1)}, u32[]{:S(2)}, u32[]{:S(2)}) collective-permute-start(f32[2,176,8]{1,0,2:T(2,128)S(1)} %get-tuple-element.28), channel_id=1, source_target_pairs={{1,0},{2,1},{3,2},{4,3},{5,4},{6,5},{7,6},{0,7},{9,8},{10,9},{11,1... | collective-permute-start | bytes 33800 | tf_op jit(solution)/shard_map/ppermute | solution.py:22
  103.7 1.4 copy-start.3
  104.0 2.2 copy-start.4
